TPU v7x, 32 devices: a whole 2x2x4 slice. The times are simulated.
32 devices in a mesh: rows: 4 (over z), tp: 4 (over y, x), unit: 2 (over core).
Axes of the slice: x: 2, y: 2, z: 4, core: 2. Of those that a mesh axis runs over, the one named last changes fastest.
Arguments:
- train_query: bfloat16 [4096, 2048], P(('unit', 'rows'), 'tp'), parts along dimension 0, may hold values from -0.125 to 0.125
- low_query: bfloat16 [4096, 64], P(('unit', 'rows')), parts along dimension 0, may hold values from -0.125 to 0.125
- high_query: bfloat16 [128, 2048], P('unit', 'tp'), parts along dimension 0, may hold values from -0.75 to 0.75
- train_key: bfloat16 [4096, 512], P(('unit', 'rows'), 'tp'), parts along dimension 0, may hold values from -0.125 to 0.125
- low_key: bfloat16 [4096, 64], P(('unit', 'rows')), parts along dimension 0, may hold values from -0.125 to 0.125
- high_key: bfloat16 [128, 512], P('unit', 'tp'), parts along dimension 0, may hold values from -0.75 to 0.75
- train_value: bfloat16 [4096, 512], P(('unit', 'rows'), 'tp'), parts along dimension 0, may hold values from -0.125 to 0.125
- low_value: bfloat16 [4096, 64], P(('unit', 'rows')), parts along dimension 0, may hold values from -0.125 to 0.125
- high_value: bfloat16 [128, 512], P('unit', 'tp'), parts along dimension 0, may hold values from -0.75 to 0.75
- norm_train: float32 [4096], P(('unit', 'rows', 'tp')), parts along dimension 0, may hold values from 0.25 to 1.75
- norm_step: float32 [4096], P(('unit', 'rows', 'tp')), parts along dimension 0, may hold values from -0.3 to 0.3
Outputs:
- final_query: bfloat16 [4096, 2048], P(('unit', 'tp')), parts along dimension 0
- final_key: bfloat16 [1024, 2048], P(('unit', 'tp')), parts along dimension 0
- final_value: bfloat16 [1024, 2048], P(('unit', 'tp')), parts along dimension 0
- serve_norm: bfloat16 [4096], P('unit'), parts along dimension 0
There are 2 independent parts, one for each index of `unit`. A program takes and returns all parts, laid end to end along the dimension named above; each array names one. Nothing has to cross between parts.
All inputs are finite; a program needn't handle non-finite values.
Results may differ from a plain program's by a relative error of at most 0.001.
Values may be sent and summed in bfloat16 or wider, within the bound.
A program may use at most 64 MiB of HBM per device.

v0:
```python
import jax
import jax.numpy as jnp
from jax import lax
from jax.sharding import PartitionSpec as P

mix_rate = 0.5


def shards(
    train_query,
    low_query,
    high_query,
    train_key,
    low_key,
    high_key,
    train_value,
    low_value,
    high_value,
    norm_train,
    norm_step,
):
    result_query = train_query.astype(jnp.float32) + mix_rate * jnp.dot(
        low_query, high_query, preferred_element_type=jnp.float32
    )
    result_key = train_key.astype(jnp.float32) + mix_rate * jnp.dot(
        low_key, high_key, preferred_element_type=jnp.float32
    )
    result_value = train_value.astype(jnp.float32) + mix_rate * jnp.dot(
        low_value, high_value, preferred_element_type=jnp.float32
    )
    narrow_query, narrow_key, narrow_value = (
        result_query.astype(jnp.bfloat16),
        result_key.astype(jnp.bfloat16),
        result_value.astype(jnp.bfloat16),
    )
    final_query, final_key, final_value = (
        lax.all_gather(narrow_query, "rows", axis=0, tiled=True),
        lax.all_gather(narrow_key, "rows", axis=0, tiled=True),
        lax.all_gather(narrow_value, "rows", axis=0, tiled=True),
    )
    final_query, final_key, final_value = (final_query.T, final_key.T, final_value.T)
    serve_norm = lax.all_gather(
        (norm_train + norm_step).astype(jnp.bfloat16), ("rows", "tp"), axis=0, tiled=True
    )
    return (final_query, final_key, final_value, serve_norm)


def solution(mesh):
    in_specs = (
        P(("unit", "rows"), "tp"),
        P(("unit", "rows"), None),
        P("unit", "tp"),
        P(("unit", "rows"), "tp"),
        P(("unit", "rows"), None),
        P("unit", "tp"),
        P(("unit", "rows"), "tp"),
        P(("unit", "rows"), None),
        P("unit", "tp"),
        P(("unit", "rows", "tp")),
        P(("unit", "rows", "tp")),
    )
    out_specs = (
        P(("unit", "tp"), None),
        P(("unit", "tp"), None),
        P(("unit", "tp"), None),
        P("unit"),
    )
    return jax.shard_map(shards, mesh=mesh, in_specs=in_specs, out_specs=out_specs, check_vma=False)
```

profile of v0, /device:TPU:0, one launch (start us, length us, event | category | flops | bytes accessed | tf_op | source)
XLA Modules:
  0.0 108.7 jit_solution(17795586656834404858)
XLA Ops:
  7.2 0.0 copy-start
  7.2 0.0 copy-start.1
  7.2 0.0 copy-start.2
  7.2 0.0 copy-start.3
  7.2 0.0 all-gather.3.cloned.1.call-start
  7.3 0.8 copy-done
  8.0 2.2 %fusion.1 = bf16[512,512]{1,0:T(8,128)(2,1)} fusion(bf16[512,64]{0,1:T(8,128)(2,1)S(1)} %copy-done, bf16[64,512]{1,0:T(8,128)(2,1)} %param.13, bf16[512,512]{1,0:T(8,128)(2,1)} %param.11), kind=kOutput, calls=%fused_computation.2 | convolution fusion | flops 34603008 | bytes 1179648 | tf_op jit(solution)/shard_map/dot_general | solution.py:22
  10.2 0.0 all-gather.3.cloned.1.call-update
  10.2 0.0 copy-start.4
  10.2 0.0 copy-start.5
  10.3 1.2 %fusion.4 = bf16[512,128]{1,0:T(8,128)(2,1)S(1)} fusion(bf16[512,64]{0,1:T(8,128)(2,1)} %param.15, bf16[64,128]{1,0:T(8,128)(2,1)} %param.16, bf16[512,128]{1,0:T(8,128)(2,1)} %param.14), kind=kOutput, calls=%fused_computation.7 | convolution fusion | flops 8650752 | bytes 344064 | tf_op jit(solution)/shard_map/dot_general | solution.py:25
  11.4 22.0 %all_gather.13 = bf16[2048,128]{1,0:T(8,128)(2,1)S(1)} all-gather(bf16[512,128]{1,0:T(8,128)(2,1)S(1)} %fusion.4), channel_id=1, replica_groups=mesh['rows'=4,'tp'=4,'unit'=2] {'rows'}, dimensions={0}, use_global_device_ids=true | all-gather | bytes 655360 | tf_op jit(solution)/shard_map/all_gather | solution.py:38
  33.4 1.0 copy.22
  34.4 0.0 copy-done.1
  34.5 0.0 copy-done.2
  34.5 0.0 copy-done.3
  34.5 0.2 fusion.5
  34.7 21.7 %all_gather.14 = bf16[2048,128]{1,0:T(8,128)(2,1)S(1)} all-gather(bf16[512,128]{1,0:T(8,128)(2,1)S(1)} %fusion.5), channel_id=1, replica_groups=mesh['rows'=4,'tp'=4,'unit'=2] {'rows'}, dimensions={0}, use_global_device_ids=true | all-gather | bytes 655360 | tf_op jit(solution)/shard_map/all_gather | solution.py:39
  56.4 1.0 copy.23
  57.4 0.0 copy-done.4
  57.4 0.0 copy-done.5
  57.4 39.9 %all-gather = bf16[16,1,128]{2,1,0:T(2,128)(2,1)S(1)} all-gather(bf16[1,1,128]{2,1,0:T(2,128)(2,1)S(1)} %convert_bitcast_fusion), channel_id=1, replica_groups=mesh['rows'=4,'tp'=4,'unit'=2] {'rows','tp'}, dimensions={0}, use_global_device_ids=true | all-gather | bytes 4352 | tf_op jit(solution)/shard_map/all_gather | solution.py:42
  97.3 0.6 reduce
  98.0 0.0 all-gather.3.cloned.1.call-done
  98.0 3.9 %copy.21 = bf16[512,2048]{1,0:T(8,128)(2,1)} copy(bf16[512,2048]{0,1:T(8,128)(2,1)} %bitcast.14) | data formatting | bytes 4194304
  (1 shorter events, 0.0 us)
Async XLA Ops:
  7.2 0.8 copy-start
  7.2 27.3 %copy-start.1 = (bf16[512,128]{1,0:T(8,128)(2,1)S(1)}, bf16[512,128]{1,0:T(8,128)(2,1)}, u32[]{:S(2)}) copy-start(bf16[512,128]{1,0:T(8,128)(2,1)} %param.17) | copy-start | bytes 393220
  7.2 27.3 %copy-start.2 = (bf16[512,64]{0,1:T(8,128)(2,1)S(1)}, bf16[512,64]{0,1:T(8,128)(2,1)}, u32[]{:S(2)}) copy-start(bf16[512,64]{0,1:T(8,128)(2,1)} %param.18) | copy-start | bytes 196612
  7.2 27.3 %copy-start.3 = (bf16[64,128]{1,0:T(8,128)(2,1)S(1)}, bf16[64,128]{1,0:T(8,128)(2,1)}, u32[]{:S(2)}) copy-start(bf16[64,128]{1,0:T(8,128)(2,1)} %param.19) | copy-start | bytes 49156
  7.2 90.7 %all-gather.3.cloned.1.call-start = ((), (), s32[]{:S(2)}) async-start(), calls=%async_computation | async-start | bytes 2621440 | tf_op jit(solution)/shard_map/all_gather | solution.py:37
  10.2 47.2 %copy-start.4 = (f32[128]{0:T(128)S(1)}, f32[128]{0:T(128)}, u32[]{:S(2)}) copy-start(f32[128]{0:T(128)} %param.20) | copy-start | bytes 1540
  10.2 47.2 %copy-start.5 = (f32[128]{0:T(128)S(1)}, f32[128]{0:T(128)}, u32[]{:S(2)}) copy-start(f32[128]{0:T(128)} %param.21) | copy-start | bytes 1540
Sparse Core Ops, SparseCore 0:
  10.3 60.1 all-gather.2
where the time goes:
time: 109 us
  blocking collectives  83.6 us (77%)
  between operations  14.1 us (13%)
  local copies, waits for them, and re-layouts  6.71 us (6%)
  matrix products  3.58 us (3%)
    all_gather x1, blocking collectives, shards(): lax.all_gather((norm_train + norm_step).astype(jnp.bfloat16), ('rows', 't...  39.9 us
    all_gather x1, blocking collectives, shards(): lax.all_gather(narrow_key, 'rows', axis=0, tiled=True)  22 us
    all_gather x1, blocking collectives, shards(): lax.all_gather(narrow_value, 'rows', axis=0, tiled=True)  21.7 us
    unnamed x15, local copies, waits for them, and re-layouts  6.71 us
    dot_general x1, matrix products, shards(): jnp.dot(low_query, high_query, preferred_element_type=jnp.float32)  2.19 us
  transfers between devices with their start and end apart: 1, of which 0 were waited for; matrix products, arithmetic and copies ran while one was open for 4% of the time, Pallas kernels for 0%

commit v1 on v0

--- a/solution.py
+++ b/solution.py
@@ -39,8 +39,16 @@
         lax.all_gather(narrow_value, "rows", axis=0, tiled=True),
     )
     final_query, final_key, final_value = (final_query.T, final_key.T, final_value.T)
-    serve_norm = lax.all_gather(
-        (norm_train + norm_step).astype(jnp.bfloat16), ("rows", "tp"), axis=0, tiled=True
+    serve_norm = jnp.concatenate(
+        lax.all_to_all(
+            jnp.stack(
+                [(norm_train + norm_step).astype(jnp.bfloat16)] * lax.axis_size(("rows", "tp"))
+            ),
+            ("rows", "tp"),
+            0,
+            0,
+        ),
+        axis=0,
     )
     return (final_query, final_key, final_value, serve_norm)
 

time: 109 us -> 86.7 us (0.80)
  blocking collectives: 83.6 us -> 45.5 us
  starting transfers between devices: 0.04 us -> 8.38 us
  waiting for transfers between devices: 0.02 us -> 6.28 us
    all_gather x1 -> x0, blocking collectives: 39.9 us -> none  [shards(): lax.all_gather((norm_train + norm_step).astype(jnp.bfloat16), ('rows', 't...]
    all_to_all x0 -> x1, starting transfers between devices: none -> 8.34 us  [shards(): lax.all_to_all(jnp.stack([(norm_train + norm_step).astype(jnp.bfloat16)]...]
    all_gather x1, waiting for transfers between devices: 0.01 us -> 6.26 us  [shards(): lax.all_gather(narrow_query, 'rows', axis=0, tiled=True)]
    all_gather x1, blocking collectives: 22 us -> 23.2 us  [shards(): lax.all_gather(narrow_key, 'rows', axis=0, tiled=True)]
    unnamed x15 -> x11, local copies, waits for them, and re-layouts: 6.71 us -> 6.7 us
  transfers between devices with their start and end apart: 1 -> 2, of which waited for: 0 -> 1; matrix products, arithmetic and copies ran while one was open for 4% -> 6% of each run, Pallas kernels for 0% -> 0%
where the time goes in v1:
time: 86.7 us; the launch traced here: 86.4 us
  blocking collectives  45.5 us (52%)
  between operations  14.1 us (16%)
  starting transfers between devices  8.38 us (10%)
  local copies, waits for them, and re-layouts  7.29 us (8%)
  waiting for transfers between devices  6.28 us (7%)
  matrix products  3.6 us (4%)
  other arithmetic  1.3 us (1%)
    all_gather x1, blocking collectives, shards(): lax.all_gather(narrow_key, 'rows', axis=0, tiled=True)  23.2 us
    all_gather x1, blocking collectives, shards(): lax.all_gather(narrow_value, 'rows', axis=0, tiled=True)  22.3 us
    all_to_all x1, starting transfers between devices, shards(): lax.all_to_all(jnp.stack([(norm_train + norm_step).astype(jnp.bfloat16)]...  8.34 us
    unnamed x11, local copies, waits for them, and re-layouts  6.7 us
    all_gather x1, waiting for transfers between devices, shards(): lax.all_gather(narrow_query, 'rows', axis=0, tiled=True)  6.26 us
    dot_general x1, matrix products, shards(): jnp.dot(low_query, high_query, preferred_element_type=jnp.float32)  2.19 us
  transfers between devices with their start and end apart: 2, of which 1 were waited for; matrix products, arithmetic and copies ran while one was open for 6% of the time, Pallas kernels for 0%

profile of v1, /device:TPU:0, one launch (start us, length us, event | category | flops | bytes accessed | tf_op | source)
XLA Modules:
  0.0 86.4 jit_solution(15022940838301561241)
XLA Ops:
  7.2 0.0 copy-start
  7.2 0.0 copy-start.1
  7.2 0.0 copy-start.2
  7.2 0.0 copy-start.3
  7.2 0.0 all-gather.2.cloned.1.call-start
  7.3 0.8 copy-done
  8.0 2.2 %fusion.1 = bf16[512,512]{1,0:T(8,128)(2,1)} fusion(bf16[512,64]{0,1:T(8,128)(2,1)S(1)} %copy-done, bf16[64,512]{1,0:T(8,128)(2,1)} %param.13, bf16[512,512]{1,0:T(8,128)(2,1)} %param.11), kind=kOutput, calls=%fused_computation.2 | convolution fusion | flops 34603008 | bytes 1179648 | tf_op jit(solution)/shard_map/dot_general | solution.py:22
  10.2 0.0 all-gather.2.cloned.1.call-update
  10.2 0.7 add_convert_fusion
  10.9 0.6 stack.2
  11.5 8.3 %all-to-all-start = ((bf16[16,1,128]{2,1,0:T(2,128)(2,1)}), bf16[16,1,128]{2,1,0:T(2,128)(2,1)S(1)}, u32[]{:S(2)}, u32[]{:S(2)}) async-start(bf16[16,1,128]{2,1,0:T(2,128)(2,1)} %stack.2), calls=%async_computation | async-start | bytes 16384 | tf_op jit(solution)/shard_map/all_to_all | solution.py:43
  19.8 1.2 %fusion.4 = bf16[512,128]{1,0:T(8,128)(2,1)S(1)} fusion(bf16[512,64]{0,1:T(8,128)(2,1)} %param.15, bf16[64,128]{1,0:T(8,128)(2,1)} %param.16, bf16[512,128]{1,0:T(8,128)(2,1)} %param.14), kind=kOutput, calls=%fused_computation.7 | convolution fusion | flops 8650752 | bytes 344064 | tf_op jit(solution)/shard_map/dot_general | solution.py:25
  21.1 23.2 %all_gather.10 = bf16[2048,128]{1,0:T(8,128)(2,1)S(1)} all-gather(bf16[512,128]{1,0:T(8,128)(2,1)S(1)} %fusion.4), channel_id=1, replica_groups=mesh['rows'=4,'tp'=4,'unit'=2] {'rows'}, dimensions={0}, use_global_device_ids=true | all-gather | bytes 655360 | tf_op jit(solution)/shard_map/all_gather | solution.py:38
  44.2 0.0 copy-done.1
  44.2 0.0 copy-done.2
  44.2 0.0 copy-done.3
  44.2 0.2 fusion.5
  44.4 22.3 %all_gather.11 = bf16[2048,128]{1,0:T(8,128)(2,1)S(1)} all-gather(bf16[512,128]{1,0:T(8,128)(2,1)S(1)} %fusion.5), channel_id=1, replica_groups=mesh['rows'=4,'tp'=4,'unit'=2] {'rows'}, dimensions={0}, use_global_device_ids=true | all-gather | bytes 655360 | tf_op jit(solution)/shard_map/all_gather | solution.py:39
  66.8 1.0 %copy.22 = bf16[128,2048]{1,0:T(8,128)(2,1)} copy(bf16[128,2048]{0,1:T(8,128)(2,1)S(1)} %bitcast.10) | data formatting | bytes 1048576
  67.8 1.0 %copy.23 = bf16[128,2048]{1,0:T(8,128)(2,1)} copy(bf16[128,2048]{0,1:T(8,128)(2,1)S(1)} %bitcast.11) | data formatting | bytes 1048576
  68.8 0.0 all-to-all-done
  68.8 0.6 reduce
  69.4 6.3 %all-gather.2.cloned.1.call-done = bf16[2048,512]{1,0:T(8,128)(2,1)} async-done(((bf16[512,512]{1,0:T(8,128)(2,1)}), bf16[2048,512]{1,0:T(8,128)(2,1)}) %all-gather.2.cloned.1.call-update) | async-done | bytes 2097168 | tf_op jit(solution)/shard_map/all_gather | solution.py:37
  75.7 3.9 %copy.21 = bf16[512,2048]{1,0:T(8,128)(2,1)} copy(bf16[512,2048]{0,1:T(8,128)(2,1)} %bitcast.12) | data formatting | bytes 4194304
Async XLA Ops:
  7.2 0.8 copy-start
  7.2 37.0 %copy-start.1 = (bf16[512,128]{1,0:T(8,128)(2,1)S(1)}, bf16[512,128]{1,0:T(8,128)(2,1)}, u32[]{:S(2)}) copy-start(bf16[512,128]{1,0:T(8,128)(2,1)} %param.17) | copy-start | bytes 393220
  7.2 37.0 %copy-start.2 = (bf16[512,64]{0,1:T(8,128)(2,1)S(1)}, bf16[512,64]{0,1:T(8,128)(2,1)}, u32[]{:S(2)}) copy-start(bf16[512,64]{0,1:T(8,128)(2,1)} %param.18) | copy-start | bytes 196612
  7.2 37.0 %copy-start.3 = (bf16[64,128]{1,0:T(8,128)(2,1)S(1)}, bf16[64,128]{1,0:T(8,128)(2,1)}, u32[]{:S(2)}) copy-start(bf16[64,128]{1,0:T(8,128)(2,1)} %param.19) | copy-start | bytes 49156
  7.2 68.5 %all-gather.2.cloned.1.call-start = ((), (), s32[]{:S(2)}) async-start(), calls=%async_computation.1 | async-start | bytes 2621440 | tf_op jit(solution)/shard_map/all_gather | solution.py:37
  11.5 57.3 %all-to-all-start = ((bf16[16,1,128]{2,1,0:T(2,128)(2,1)}), bf16[16,1,128]{2,1,0:T(2,128)(2,1)S(1)}, u32[]{:S(2)}, u32[]{:S(2)}) async-start(bf16[16,1,128]{2,1,0:T(2,128)(2,1)} %stack.2), calls=%async_computation | async-start | bytes 16384 | tf_op jit(solution)/shard_map/all_to_all | solution.py:43
Sparse Core Ops, SparseCore 0:
  10.3 65.2 all-gather.1
